TPU v7x, 512 devices: a whole 4x8x8 slice. The times are simulated.
512 devices in a mesh: tp: 16 (over z, core), ep: 32 (over y, x).
Axes of the slice: x: 4, y: 8, z: 8, core: 2. Of those that a mesh axis runs over, the one named last changes fastest.
Arguments:
- tokens: bfloat16 [12288, 2048], P('ep', 'tp'), may hold values from -6 to 6
- norm_gain: float32 [2048], replicated, may hold values from 0.25 to 1.75
- shared_gate: bfloat16 [2048, 2816], P('ep', 'tp'), may hold values from -0.125 to 0.125
- shared_up: bfloat16 [2048, 2816], P('ep', 'tp'), may hold values from -0.125 to 0.125
- shared_down: bfloat16 [2816, 2048], P('tp', 'ep'), may hold values from -0.21875 to 0.21875
- expert_gate: bfloat16 [16, 32, 176, 2048], P('tp', 'ep'), may hold values from -0.125 to 0.125
- expert_up: bfloat16 [16, 32, 176, 2048], P('tp', 'ep'), may hold values from -0.125 to 0.125
- expert_down: bfloat16 [64, 1408, 2048], P('ep', None, 'tp'), may hold values from -0.15625 to 0.15625
- chosen: int32 [64, 384], P('ep'), may hold values from 0 to 12287, as said below
- gates: float32 [64, 384], P('ep'), may hold values from 0.1 to 1
Outputs:
- mixed: bfloat16 [12288, 2048], P('ep', 'tp')
Inputs may be any that keep to these rules, and one draw needn't show every extreme that they name: Each row of chosen holds 384 different token indices in rising order. Of one row, at most 24 lie among the 384 tokens of one index of ep (tokens s * 384 to (s + 1) * 384 - 1), and in every row exactly 24 lie among those of some index.
All inputs are finite; a program needn't handle non-finite values.
Results may differ from a plain program's by a relative error of at most 0.012.
Values may be sent and summed in bfloat16 or wider, within the bound.
A program may use at most 64 MiB of HBM per device.

v0:
```python
import jax
import jax.numpy as jnp
from jax import lax
from jax.sharding import PartitionSpec as P

EXP_DEV = 2
TOK_DEV = 384
CAP = 384
norm_eps = 1e-06


def side_by_side(arrays, axis, dim, along):
    both = jnp.concatenate(arrays, axis=along)
    whole, at, gathered = (lax.all_gather(both, axis, axis=dim, tiled=True), 0, [])
    for a in arrays:
        gathered.append(lax.slice_in_dim(whole, at, at + a.shape[along], axis=along))
        at += a.shape[along]
    return tuple(gathered)


def sent_to_all(array, axis):
    length = lax.axis_size(axis)
    return lax.all_to_all(
        jnp.broadcast_to(array[None], (length, *array.shape)), axis, 0, 0, tiled=True
    )


def joined_along(pieces, dim):
    dims = list(pieces.shape[1:])
    dims[dim] *= pieces.shape[0]
    return jnp.moveaxis(pieces, 0, dim).reshape(dims)


def gathered_copies(array, axis, dim):
    pieces = sent_to_all(array, axis)
    return joined_along(pieces, dim)


def on_device(
    tokens,
    norm_gain,
    shared_gate,
    shared_up,
    shared_down,
    expert_gate,
    expert_up,
    expert_down,
    chosen,
    gates,
):
    tp_count = lax.axis_size("tp")
    ep_count = lax.axis_size("ep")
    slice_width = tokens.shape[1]
    whole = lax.all_gather(tokens, "tp", axis=1, tiled=True)
    widened = whole.astype(jnp.float32)
    inv_scale = lax.rsqrt(jnp.mean(widened * widened, axis=1, keepdims=True) + norm_eps)
    normed = (widened * inv_scale * norm_gain).astype(jnp.bfloat16)
    pieces = side_by_side((shared_gate, shared_up), "ep", 0, 1)
    gate_sum = jnp.dot(normed, pieces[0], preferred_element_type=jnp.float32)
    up_sum = jnp.dot(normed, pieces[1], preferred_element_type=jnp.float32)
    shared_hidden = (jax.nn.silu(gate_sum) * up_sum).astype(jnp.bfloat16)
    partial_out = jnp.dot(
        shared_hidden, gathered_copies(shared_down, "ep", 1), preferred_element_type=jnp.float32
    )
    shared_part = lax.psum_scatter(
        partial_out.astype(jnp.bfloat16), "tp", scatter_dimension=1, tiled=True
    ).astype(jnp.float32)
    slot_most = 2 * CAP // ep_count
    slot_count = ep_count * slot_most
    sources = chosen // TOK_DEV
    source_flags = (
        sources[:, :, None] == jnp.arange(ep_count, dtype=jnp.int32)[None, None, :]
    ).astype(jnp.int32)
    counts = jnp.sum(source_flags, axis=1)
    starts = jnp.cumsum(counts, axis=1) - counts
    run_start = jnp.take_along_axis(starts, sources, axis=1)
    slot_index = sources * slot_most + jnp.arange(CAP, dtype=jnp.int32)[None, :] - run_start
    local_ids = chosen - sources * TOK_DEV
    expert_rows = jnp.arange(EXP_DEV, dtype=jnp.int32)[:, None]
    requests = (
        jnp.full((EXP_DEV, slot_count), TOK_DEV, jnp.int32)
        .at[expert_rows, slot_index]
        .set(local_ids)
    )
    requests = requests.reshape(EXP_DEV, ep_count, slot_most)
    asked_ids = lax.all_to_all(requests, "ep", split_axis=1, concat_axis=1, tiled=True)
    clipped = jnp.minimum(asked_ids, TOK_DEV - 1)
    local_expert = lax.axis_index("tp") // (tp_count // EXP_DEV)
    own_requests = lax.dynamic_index_in_dim(clipped, local_expert, 0, keepdims=False)
    outgoing = jnp.take(normed, own_requests.reshape(-1), axis=0).reshape(ep_count, slot_most, -1)
    arrived = lax.all_to_all(outgoing, "ep", split_axis=0, concat_axis=0, tiled=True)
    token_rows = arrived.reshape(slot_count, -1)
    gate_weight = expert_gate.reshape(expert_gate.shape[2], expert_gate.shape[3])
    up_weight = expert_up.reshape(expert_up.shape[2], expert_up.shape[3])
    gate_values = jnp.einsum(
        "hd,rd->hr", gate_weight, token_rows, preferred_element_type=jnp.float32
    )
    up_values = jnp.einsum("hd,rd->hr", up_weight, token_rows, preferred_element_type=jnp.float32)
    part_hidden = (jax.nn.silu(gate_values) * up_values).astype(jnp.bfloat16)
    all_hidden = lax.all_gather(part_hidden, "tp", axis=0, tiled=True)
    width_hidden = expert_down.shape[1]
    placed_rows = []
    for expert_slot in range(EXP_DEV):
        hidden_block = all_hidden[expert_slot * width_hidden : (expert_slot + 1) * width_hidden, :]
        outputs = jnp.einsum(
            "fr,fd->rd", hidden_block, expert_down[expert_slot], preferred_element_type=jnp.float32
        )
        gate_slots = (
            jnp.zeros((slot_count,), jnp.float32)
            .at[slot_index[expert_slot]]
            .set(gates[expert_slot])
        )
        placed = (gate_slots[:, None] * outputs).astype(jnp.bfloat16)
        placed_rows.append(placed)
    stacked = jnp.stack(placed_rows).reshape(EXP_DEV, ep_count, slot_most, slice_width)
    returned = lax.all_to_all(stacked, "ep", split_axis=1, concat_axis=1, tiled=True)
    flat_values = returned.reshape(-1, slice_width)
    flat_ids = asked_ids.reshape(-1)
    picker = (jnp.arange(TOK_DEV, dtype=jnp.int32)[:, None] == flat_ids[None, :]).astype(
        jnp.bfloat16
    )
    routed = jnp.dot(picker, flat_values, preferred_element_type=jnp.float32)
    return (shared_part + routed).astype(jnp.bfloat16)


def solution(mesh):
    return jax.shard_map(
        on_device,
        mesh=mesh,
        in_specs=(
            P("ep", "tp"),
            P(),
            P("ep", "tp"),
            P("ep", "tp"),
            P("tp", "ep"),
            P("tp", "ep", None, None),
            P("tp", "ep", None, None),
            P("ep", None, "tp"),
            P("ep", None),
            P("ep", None),
        ),
        out_specs=P("ep", "tp"),
        check_vma=False,
    )
```

profile of v0, /device:TPU:4, one launch (start us, length us, event | category | flops | bytes accessed | tf_op | source)
XLA Modules:
  0.0 284.9 jit_solution(4781293270764742484)
XLA Ops:
  7.4 0.7 all-gather.4.cloned.1.call-update
  8.1 0.7 multiply_subtract_fusion
  8.8 0.1 convert_reduce_fusion
  8.9 0.2 reduce_window_sum.11
  9.2 6.6 %gather_fusion.1 = s32[768]{0:T(1024)S(1)} fusion(s32[2,32]{1,0:T(2,128)S(1)} %sub.20, s32[768]{0:T(1024)S(1)} %reshape.168), kind=kCustom, calls=%fused_computation.1 | custom fusion | bytes 12288 | tf_op jit(solution)/shard_map/jit(take_along_axis)/gather | solution.py:76
  15.9 36.5 %scatter_fusion = s32[2,768]{1,0:T(2,128)S(1)} fusion(s32[2,768]{1,0:T(2,128)S(1)} %broadcast_in_dim.23, s32[768]{0:T(1024)S(1)} %reshape.174, s32[768]{0:T(1024)S(1)} %reshape.176), kind=kCustom, calls=%fused_computation.2 | custom fusion | bytes 15360 | tf_op jit(solution)/shard_map/scatter | solution.py:83
  52.3 0.1 reshape.153
  52.4 0.6 copy.21
  53.1 10.2 %all-to-all-start.1 = ((s32[2,32,24]{2,0,1:T(2,128)}), s32[2,32,24]{2,0,1:T(2,128)S(1)}, u32[]{:S(2)}, u32[]{:S(2)}) async-start(s32[2,32,24]{2,0,1:T(2,128)} %copy.21), calls=%async_computation.1 | async-start | bytes 65536 | tf_op jit(solution)/shard_map/all_to_all | solution.py:86
  63.3 7.8 %all-to-all-done.1 = s32[2,32,24]{2,0,1:T(2,128)S(1)} async-done(((s32[2,32,24]{2,0,1:T(2,128)}), s32[2,32,24]{2,0,1:T(2,128)S(1)}, u32[]{:S(2)}, u32[]{:S(2)}) %all-to-all-start.1) | async-done | bytes 6176 | tf_op jit(solution)/shard_map/all_to_all | solution.py:86
  71.2 0.5 broadcast.160
  71.7 0.7 fusion.55
  72.4 0.1 reshape.155
  72.5 0.0 all-gather.4.cloned.1.call-done
  72.6 1.9 fusion
  74.5 0.4 fusion.2
  74.9 4.3 %gather_fusion = bf16[768,2048]{1,0:T(8,128)(2,1)} fusion(bf16[384,2048]{1,0:T(8,128)(2,1)S(1)} %fusion.2, s32[1024]{0:T(1024)S(1)} %pad_clamp_fusion), kind=kCustom, calls=%fused_computation | custom fusion | bytes 6294528 | tf_op jit(solution)/shard_map/jit(_take)/gather | solution.py:90
  79.2 3.9 %broadcast_select_fusion = bf16[32,24,2048]{2,1,0:T(8,128)(2,1)} fusion(bf16[32,24,2048]{2,1,0:T(8,128)(2,1)} %bitcast.63, pred[32,24]{1,0:T(8,128)(4,1)S(1)} %compare_and_fusion), kind=kLoop, calls=%fused_computation.10 | loop fusion | flops 1572864 | bytes 6292224 | tf_op jit(solution)/shard_map/jit(_take)/select_n | solution.py:90
  83.1 6.8 %all-to-all-start.2 = ((bf16[32,24,2048]{2,1,0:T(8,128)(2,1)}), bf16[32,24,2048]{2,1,0:T(8,128)(2,1)}, u32[]{:S(2)}, u32[]{:S(2)}) async-start(bf16[32,24,2048]{2,1,0:T(8,128)(2,1)} %broadcast_select_fusion), calls=%async_computation.2 | async-start | bytes 6291456 | tf_op jit(solution)/shard_map/all_to_all | solution.py:91
  89.9 0.0 all-gather.6.cloned.1.call-start
  90.0 0.7 pad_maximum_fusion.1
  90.7 0.0 all-gather.6.cloned.1.call-update
  90.7 0.0 all-gather.8.cloned.1.call-start
  90.8 73.0 %all-to-all-done.2 = bf16[32,24,2048]{2,1,0:T(8,128)(2,1)} async-done(((bf16[32,24,2048]{2,1,0:T(8,128)(2,1)}), bf16[32,24,2048]{2,1,0:T(8,128)(2,1)}, u32[]{:S(2)}, u32[]{:S(2)}) %all-to-all-start.2) | async-done | bytes 3145760 | tf_op jit(solution)/shard_map/all_to_all | solution.py:91
  163.8 3.2 %convolution_bitcast_fusion.1 = f32[176,768]{1,0:T(8,128)S(1)} fusion(bf16[768,2048]{1,0:T(8,128)(2,1)} %bitcast.7, bf16[1,1,176,2048]{3,2,1,0:T(8,128)(2,1)S(1)} %copy-done), kind=kOutput, calls=%fused_computation.19 | convolution fusion | flops 553648128 | bytes 4407296 | tf_op jit(solution)/shard_map/hd,rd->hr/dot_general | solution.py:95
  167.0 3.8 %fusion.9 = bf16[176,768]{1,0:T(8,128)(2,1)} fusion(bf16[768,2048]{1,0:T(8,128)(2,1)} %bitcast.7, bf16[1,1,176,2048]{3,2,1,0:T(8,128)(2,1)S(1)} %copy-done.8, f32[176,768]{1,0:T(8,128)S(1)} %convolution_bitcast_fusion.1), kind=kOutput, calls=%fused_computation.21 | convolution fusion | flops 554459136 | bytes 4677632 | tf_op jit(solution)/shard_map/hd,rd->hr/dot_general | solution.py:98
  170.8 0.0 all-gather.8.cloned.1.call-update
  170.9 1.1 broadcast_in_dim.19
  172.0 5.5 %all-to-all-start = ((bf16[32,176,64]{1,2,0:T(8,128)(2,1)}), bf16[32,176,64]{1,2,0:T(8,128)(2,1)S(1)}, u32[]{:S(2)}, u32[]{:S(2)}) async-start(bf16[32,176,64]{1,2,0:T(8,128)(2,1)} %broadcast_in_dim.19), calls=%async_computation | async-start | bytes 2097152 | tf_op jit(solution)/shard_map/all_to_all | solution.py:23
  177.5 0.0 reduce-scatter.4.cloned.1.call-start
  177.5 9.4 %all-gather.6.cloned.1.call-done = bf16[2048,352]{1,0:T(8,128)(2,1)} async-done(((bf16[64,352]{1,0:T(8,128)(2,1)}), bf16[2048,352]{1,0:T(8,128)(2,1)}) %all-gather.6.cloned.1.call-update) | async-done | bytes 1441808 | tf_op jit(solution)/shard_map/all_gather | solution.py:14
  186.9 2.6 fusion.28
  189.5 14.7 %all-to-all-done = bf16[32,176,64]{1,2,0:T(8,128)(2,1)S(1)} async-done(((bf16[32,176,64]{1,2,0:T(8,128)(2,1)}), bf16[32,176,64]{1,2,0:T(8,128)(2,1)S(1)}, u32[]{:S(2)}, u32[]{:S(2)}) %all-to-all-start) | async-done | bytes 720928 | tf_op jit(solution)/shard_map/all_to_all | solution.py:23
  204.2 4.3 %convolution_convert_fusion = bf16[384,2048]{1,0:T(8,128)(2,1)} fusion(bf16[176,2048]{0,1:T(8,128)(2,1)S(1)} %bitcast.65, bf16[384,2048]{1,0:T(8,128)(2,1)S(1)} %fusion.2, bf16[2048,352]{1,0:T(8,128)(2,1)} %all-gather.6.cloned.1.call-done, f32[384,176]{0,1:T(8,128)} %fusion.28), kind=kOutput, calls=%fused_computation.11 | convolution fusion | flops 554840064 | bytes 5185536 | tf_op jit(solution)/shard_map/dot_general | solution.py:62
  208.5 2.7 copy.26
  211.2 0.0 reduce-scatter.4.cloned.1.call-update
  211.3 3.1 %scatter_custom_fusion.1 = f32[768]{0:T(1024)S(1)} fusion(s32[384]{0:T(512)S(1)} %get-tuple-element.7, f32[384]{0:T(512)S(1)} %get-tuple-element.5, f32[]{:T(128)} %constant.48.clone.1), kind=kCustom, calls=%fused_computation.73 | custom fusion | bytes 3076 | tf_op jit(solution)/shard_map/scatter | solution.py:111
  214.4 2.9 %scatter_custom_fusion.2 = f32[768]{0:T(1024)S(1)} fusion(s32[384]{0:T(512)S(1)} %get-tuple-element.8, f32[384]{0:T(512)S(1)} %get-tuple-element.6, f32[]{:T(128)} %constant.48.clone.1), kind=kCustom, calls=%fused_computation.71 | custom fusion | bytes 3076 | tf_op jit(solution)/shard_map/scatter | solution.py:111
  217.3 16.4 %all-gather.8.cloned.1.call-done = bf16[2816,768]{1,0:T(8,128)(2,1)} async-done(((bf16[176,768]{1,0:T(8,128)(2,1)}), bf16[2816,768]{1,0:T(8,128)(2,1)}) %all-gather.8.cloned.1.call-update) | async-done | bytes 4325392 | tf_op jit(solution)/shard_map/all_gather | solution.py:100
  233.8 2.5 fusion.17
  236.3 0.3 copy-done.7
  236.7 0.8 fusion.20
  237.4 0.8 pad_maximum_fusion
  238.2 9.9 %all-to-all-start.3 = ((bf16[2,32,24,128]{3,2,0,1:T(8,128)(2,1)}), bf16[2,32,24,128]{3,2,0,1:T(8,128)(2,1)S(1)}, u32[]{:S(2)}, u32[]{:S(2)}) async-start(bf16[2,32,24,128]{3,2,0,1:T(8,128)(2,1)} %pad_maximum_fusion), calls=%async_computation.3 | async-start | bytes 786432 | tf_op jit(solution)/shard_map/all_to_all | solution.py:116
  248.1 0.1 eq.32
  248.2 27.1 %reduce-scatter.4.cloned.1.call-done = bf16[128,384]{1,0:T(8,128)(2,1)} async-done(((bf16[2048,384]{1,0:T(8,128)(2,1)}), bf16[128,384]{1,0:T(8,128)(2,1)}) %reduce-scatter.4.cloned.1.call-update) | async-done | bytes 98320
  275.3 1.0 copy.27
  276.3 1.2 fusion.25
  (37 shorter events, 0.2 us)
Async XLA Ops:
  7.4 156.5 %copy-start = (bf16[1,1,176,2048]{3,2,1,0:T(8,128)(2,1)S(1)}, bf16[1,1,176,2048]{3,2,1,0:T(8,128)(2,1)}, u32[]{:S(2)}) copy-start(bf16[1,1,176,2048]{3,2,1,0:T(8,128)(2,1)} %param.15) | copy-start | bytes 2162692
  7.4 65.2 %all-gather.4.cloned.1.call-start = ((), (), s32[]{:S(2)}) async-start(), calls=%async_computation.5 | async-start | bytes 1671168 | tf_op jit(solution)/shard_map/all_gather | solution.py:54
  15.8 58.6 %copy-start.5 = (f32[2048]{0:T(1024)S(1)}, f32[2048]{0:T(1024)}, u32[]{:S(2)}) copy-start(f32[2048]{0:T(1024)} %param.11) | copy-start | bytes 24580
  53.1 18.1 %all-to-all-start.1 = ((s32[2,32,24]{2,0,1:T(2,128)}), s32[2,32,24]{2,0,1:T(2,128)S(1)}, u32[]{:S(2)}, u32[]{:S(2)}) async-start(s32[2,32,24]{2,0,1:T(2,128)} %copy.21), calls=%async_computation.1 | async-start | bytes 65536 | tf_op jit(solution)/shard_map/all_to_all | solution.py:86
  72.6 1.9 copy-start.1
  83.1 6.9 %copy-start.2 = (bf16[64,176]{1,0:T(8,128)(2,1)S(1)}, bf16[64,176]{1,0:T(8,128)(2,1)}, u32[]{:S(2)}) copy-start(bf16[64,176]{1,0:T(8,128)(2,1)} %param.13) | copy-start | bytes 67588
  83.1 6.9 %copy-start.3 = (bf16[64,176]{1,0:T(8,128)(2,1)S(1)}, bf16[64,176]{1,0:T(8,128)(2,1)}, u32[]{:S(2)}) copy-start(bf16[64,176]{1,0:T(8,128)(2,1)} %param.12) | copy-start | bytes 67588
  83.1 80.7 %all-to-all-start.2 = ((bf16[32,24,2048]{2,1,0:T(8,128)(2,1)}), bf16[32,24,2048]{2,1,0:T(8,128)(2,1)}, u32[]{:S(2)}, u32[]{:S(2)}) async-start(bf16[32,24,2048]{2,1,0:T(8,128)(2,1)} %broadcast_select_fusion), calls=%async_computation.2 | async-start | bytes 6291456 | tf_op jit(solution)/shard_map/all_to_all | solution.py:91
  89.9 97.0 %all-gather.6.cloned.1.call-start = ((), (), s32[]{:S(2)}) async-start(), calls=%async_computation.6 | async-start | bytes 1622016 | tf_op jit(solution)/shard_map/all_gather | solution.py:14
  90.7 143.0 %all-gather.8.cloned.1.call-start = ((), (), s32[]{:S(2)}) async-start(), calls=%async_computation.7 | async-start | bytes 4595712 | tf_op jit(solution)/shard_map/all_gather | solution.py:100
  163.8 3.2 %copy-start.8 = (bf16[1,1,176,2048]{3,2,1,0:T(8,128)(2,1)S(1)}, bf16[1,1,176,2048]{3,2,1,0:T(8,128)(2,1)}, u32[]{:S(2)}) copy-start(bf16[1,1,176,2048]{3,2,1,0:T(8,128)(2,1)} %param.16) | copy-start | bytes 2162692
  167.0 3.8 %copy-start.4 = (bf16[176,64]{0,1:T(8,128)(2,1)S(1)}, bf16[176,64]{0,1:T(8,128)(2,1)}, u32[]{:S(2)}) copy-start(bf16[176,64]{0,1:T(8,128)(2,1)} %param.14) | copy-start | bytes 67588
  172.0 32.2 %all-to-all-start = ((bf16[32,176,64]{1,2,0:T(8,128)(2,1)}), bf16[32,176,64]{1,2,0:T(8,128)(2,1)S(1)}, u32[]{:S(2)}, u32[]{:S(2)}) async-start(bf16[32,176,64]{1,2,0:T(8,128)(2,1)} %broadcast_in_dim.19), calls=%async_computation | async-start | bytes 2097152 | tf_op jit(solution)/shard_map/all_to_all | solution.py:23
  177.5 97.8 %reduce-scatter.4.cloned.1.call-start = ((), (), s32[]{:S(2)}) async-start(), calls=%async_computation.8 | async-start | bytes 1671168
  208.5 2.7 copy-start.6
  208.5 25.3 %copy-start.9 = (bf16[2,1408,128]{2,1,0:T(8,128)(2,1)S(1)}, bf16[2,1408,128]{2,1,0:T(8,128)(2,1)}, u32[]{:S(2)}) copy-start(bf16[2,1408,128]{2,1,0:T(8,128)(2,1)} %param.17) | copy-start | bytes 2162692
  233.8 2.9 %copy-start.7 = (bf16[2816,768]{1,0:T(8,128)(2,1)S(1)}, bf16[2816,768]{1,0:T(8,128)(2,1)}, u32[]{:S(2)}) copy-start(bf16[2816,768]{1,0:T(8,128)(2,1)} %all-gather.8.cloned.1.call-done) | copy-start | bytes 12976132
  238.2 38.1 %all-to-all-start.3 = ((bf16[2,32,24,128]{3,2,0,1:T(8,128)(2,1)}), bf16[2,32,24,128]{3,2,0,1:T(8,128)(2,1)S(1)}, u32[]{:S(2)}, u32[]{:S(2)}) async-start(bf16[2,32,24,128]{3,2,0,1:T(8,128)(2,1)} %pad_maximum_fusion), calls=%async_computation.3 | async-start | bytes 786432 | tf_op jit(solution)/shard_map/all_to_all | solution.py:116
Sparse Core Ops, SparseCore 0:
  10.2 46.8 all-gather.3
  211.4 63.8 reduce-scatter.3
Sparse Core Ops, SparseCore 1:
  93.6 93.3 all-gather.5
  188.9 44.8 all-gather.7
where the time goes:
time: 286 us; the launch traced here: 285 us
  waiting for transfers between devices  149 us (52%)
  local copies, waits for them, and re-layouts  60.1 us (21%)
  starting transfers between devices  32.5 us (11%)
  matrix products  18.4 us (6%)
  between operations  15.2 us (5%)
  other arithmetic  9.57 us (3%)
    all_to_all x1, waiting for transfers between devices, on_device(): lax.all_to_all(outgoing, 'ep', split_axis=0, concat_axis=0, tiled=True)  73 us
    scatter x1, local copies, waits for them, and re-layouts, on_device(): requests = jnp.full((EXP_DEV, slot_count), TOK_DEV, jnp.int32).at[expert_...  36.5 us
    unnamed x5, waiting for transfers between devices  27.8 us
    all_gather x1, waiting for transfers between devices, on_device(): all_hidden = lax.all_gather(part_hidden, 'tp', axis=0, tiled=True)  16.4 us
    all_to_all x1, waiting for transfers between devices, sent_to_all(): lax.all_to_all(jnp.broadcast_to(array[None], (length, *array.shape)), axi...  14.7 us
    all_to_all x1, starting transfers between devices, on_device(): lax.all_to_all(requests, 'ep', split_axis=1, concat_axis=1, tiled=True)  10.2 us
    all_to_all x1, starting transfers between devices, on_device(): lax.all_to_all(stacked, 'ep', split_axis=1, concat_axis=1, tiled=True)  9.87 us
    all_gather x1, waiting for transfers between devices, side_by_side(): lax.all_gather(both, axis, axis=dim, tiled=True)  9.39 us
  transfers between devices with their start and end apart: 8, of which 6 were waited for; matrix products, arithmetic and copies ran while one was open for 27% of the time, Pallas kernels for 0%

commit v1 on v0

--- a/solution.py
+++ b/solution.py
@@ -7,6 +7,27 @@
 TOK_DEV = 384
 CAP = 384
 norm_eps = 1e-06
+
+
+def put_target(xs):
+    total_devices = jax.lax.axis_size("tp")
+    steps_seen = []
+    for hop_no in tuple(range(total_devices)):
+        steps_seen.append((hop_no, (hop_no + 1) % total_devices))
+    copies = []
+    for hop_no in [*range(total_devices)]:
+        copies.append((hop_no, (hop_no - 1) % total_devices))
+    u1, b_next = ([xs], [xs])
+    for _ in range(total_devices // 2):
+        u1.append(jax.lax.ppermute(u1[-1], "tp", steps_seen))
+    for _ in [*range((total_devices - 1) // 2)]:
+        earlier = jax.lax.ppermute(b_next[-1], perm=copies, axis_name="tp")
+        b_next.append(earlier)
+    return jnp.roll(
+        jnp.concatenate([*u1[::-1], *b_next[1:]], 0),
+        (jax.lax.axis_index("tp") - total_devices // 2) * xs.shape[0],
+        0,
+    )
 
 
 def side_by_side(arrays, axis, dim, along):
@@ -97,7 +118,7 @@
     )
     up_values = jnp.einsum("hd,rd->hr", up_weight, token_rows, preferred_element_type=jnp.float32)
     part_hidden = (jax.nn.silu(gate_values) * up_values).astype(jnp.bfloat16)
-    all_hidden = lax.all_gather(part_hidden, "tp", axis=0, tiled=True)
+    all_hidden = put_target(part_hidden)
     width_hidden = expert_down.shape[1]
     placed_rows = []
     for expert_slot in range(EXP_DEV):

time: 286 us -> 314 us (1.098)
  starting transfers between devices: 32.5 us -> 54 us
  local copies, waits for them, and re-layouts: 60.1 us -> 78.3 us
  waiting for transfers between devices: 149 us -> 137 us
    ppermute x0 -> x15, waiting for transfers between devices: none -> 26.5 us  [the longest x7 13.6 us: put_target(): earlier = jax.lax.ppermute(b_next[-1], perm=copies, axis_name='tp')]
    ppermute x0 -> x15, starting transfers between devices: none -> 21.8 us  [the longest x7 21.8 us: put_target(): earlier = jax.lax.ppermute(b_next[-1], perm=copies, axis_name='tp')]
    unnamed x22 -> x59, local copies, waits for them, and re-layouts: 4.1 us -> 22.2 us
    all_gather x1 -> x0, waiting for transfers between devices: 16.4 us -> none  [on_device(): all_hidden = lax.all_gather(part_hidden, 'tp', axis=0, tiled=True)]
    all_to_all x1, waiting for transfers between devices: 14.7 us -> 0.01 us  [sent_to_all(): lax.all_to_all(jnp.broadcast_to(array[None], (length, *array.shape)), axi...]
    all_gather x1, waiting for transfers between devices: 9.39 us -> 0.01 us  [side_by_side(): lax.all_gather(both, axis, axis=dim, tiled=True)]
    unnamed x5 -> x4, waiting for transfers between devices: 27.8 us -> 30 us
  transfers between devices with their start and end apart: 8 -> 22, of which waited for: 6 -> 8; matrix products, arithmetic and copies ran while one was open for 27% -> 29% of each run, Pallas kernels for 0% -> 0%
where the time goes in v1:
time: 314 us; the launch traced here: 312 us
  waiting for transfers between devices  137 us (44%)
  local copies, waits for them, and re-layouts  78.3 us (25%)
  starting transfers between devices  54 us (17%)
  matrix products  16.4 us (5%)
  between operations  15.4 us (5%)
  other arithmetic  10.8 us (3%)
    all_to_all x1, waiting for transfers between devices, on_device(): lax.all_to_all(outgoing, 'ep', split_axis=0, concat_axis=0, tiled=True)  73.1 us
    scatter x1, local copies, waits for them, and re-layouts, on_device(): requests = jnp.full((EXP_DEV, slot_count), TOK_DEV, jnp.int32).at[expert_...  36.5 us
    unnamed x4, waiting for transfers between devices  30 us
    unnamed x59, local copies, waits for them, and re-layouts  22.2 us
    ppermute x7, starting transfers between devices, put_target(): earlier = jax.lax.ppermute(b_next[-1], perm=copies, axis_name='tp')  21.8 us
    ppermute x7, waiting for transfers between devices, put_target(): earlier = jax.lax.ppermute(b_next[-1], perm=copies, axis_name='tp')  13.6 us
    ppermute x8, waiting for transfers between devices, put_target(): u1.append(jax.lax.ppermute(u1[-1], 'tp', steps_seen))  12.9 us
    all_to_all x1, starting transfers between devices, on_device(): lax.all_to_all(requests, 'ep', split_axis=1, concat_axis=1, tiled=True)  10.2 us
  transfers between devices with their start and end apart: 22, of which 8 were waited for; matrix products, arithmetic and copies ran while one was open for 29% of the time, Pallas kernels for 0%

profile of v1, /device:TPU:4, one launch (start us, length us, event | category | flops | bytes accessed | tf_op | source)
XLA Modules:
  0.0 312.4 jit_solution(16419233760693024892)
XLA Ops:
  9.2 6.6 %gather_fusion.1 = s32[768]{0:T(1024)S(1)} fusion(s32[2,32]{1,0:T(2,128)S(1)} %sub.27, s32[768]{0:T(1024)S(1)} %reshape.168), kind=kCustom, calls=%fused_computation.1 | custom fusion | bytes 12288 | tf_op jit(solution)/shard_map/jit(take_along_axis)/gather | solution.py:97
  15.8 36.5 %scatter_fusion = s32[2,768]{1,0:T(2,128)S(1)} fusion(s32[2,768]{1,0:T(2,128)S(1)} %broadcast_in_dim.23, s32[768]{0:T(1024)S(1)} %reshape.174, s32[768]{0:T(1024)S(1)} %reshape.176), kind=kCustom, calls=%fused_computation.2 | custom fusion | bytes 15360 | tf_op jit(solution)/shard_map/scatter | solution.py:104
  53.1 10.2 %all-to-all-start.1 = ((s32[2,32,24]{2,0,1:T(2,128)}), s32[2,32,24]{2,0,1:T(2,128)S(1)}, u32[]{:S(2)}, u32[]{:S(2)}) async-start(s32[2,32,24]{2,0,1:T(2,128)} %copy.21), calls=%async_computation.1 | async-start | bytes 65536 | tf_op jit(solution)/shard_map/all_to_all | solution.py:107
  63.3 7.8 %all-to-all-done.1 = s32[2,32,24]{2,0,1:T(2,128)S(1)} async-done(((s32[2,32,24]{2,0,1:T(2,128)}), s32[2,32,24]{2,0,1:T(2,128)S(1)}, u32[]{:S(2)}, u32[]{:S(2)}) %all-to-all-start.1) | async-done | bytes 6176 | tf_op jit(solution)/shard_map/all_to_all | solution.py:107
  72.6 1.8 fusion
  74.4 1.8 fusion.2
  76.2 4.3 %gather_fusion = bf16[768,2048]{1,0:T(8,128)(2,1)} fusion(bf16[384,2048]{1,0:T(8,128)(2,1)S(1)} %fusion.2, s32[1024]{0:T(1024)S(1)} %pad_clamp_fusion), kind=kCustom, calls=%fused_computation | custom fusion | bytes 6294528 | tf_op jit(solution)/shard_map/jit(_take)/gather | solution.py:111
  80.5 3.9 %broadcast_select_fusion = bf16[32,24,2048]{2,1,0:T(8,128)(2,1)} fusion(bf16[32,24,2048]{2,1,0:T(8,128)(2,1)} %bitcast.63, pred[32,24]{1,0:T(8,128)(4,1)S(1)} %compare_and_fusion), kind=kLoop, calls=%fused_computation.10 | loop fusion | flops 1572864 | bytes 6292224 | tf_op jit(solution)/shard_map/jit(_take)/select_n | solution.py:111
  84.4 6.7 %all-to-all-start.2 = ((bf16[32,24,2048]{2,1,0:T(8,128)(2,1)}), bf16[32,24,2048]{2,1,0:T(8,128)(2,1)}, u32[]{:S(2)}, u32[]{:S(2)}) async-start(bf16[32,24,2048]{2,1,0:T(8,128)(2,1)} %broadcast_select_fusion), calls=%async_computation.2 | async-start | bytes 6291456 | tf_op jit(solution)/shard_map/all_to_all | solution.py:112
  91.8 73.1 %all-to-all-done.2 = bf16[32,24,2048]{2,1,0:T(8,128)(2,1)} async-done(((bf16[32,24,2048]{2,1,0:T(8,128)(2,1)}), bf16[32,24,2048]{2,1,0:T(8,128)(2,1)}, u32[]{:S(2)}, u32[]{:S(2)}) %all-to-all-start.2) | async-done | bytes 3145760 | tf_op jit(solution)/shard_map/all_to_all | solution.py:112
  165.0 3.1 convolution_bitcast_fusion.1
  168.1 3.3 %fusion.9 = bf16[176,768]{1,0:T(8,128)(2,1)S(1)} fusion(bf16[768,2048]{1,0:T(8,128)(2,1)} %bitcast.7, bf16[1,1,176,2048]{3,2,1,0:T(8,128)(2,1)} %param.16, f32[176,768]{1,0:T(8,128)S(1)} %convolution_bitcast_fusion.1), kind=kOutput, calls=%fused_computation.21 | convolution fusion | flops 554459136 | bytes 4677632 | tf_op jit(solution)/shard_map/hd,rd->hr/dot_general | solution.py:119
  171.4 12.9 %collective-permute-done = bf16[176,768]{1,0:T(8,128)(2,1)S(1)} collective-permute-done((bf16[176,768]{1,0:T(8,128)(2,1)S(1)}, bf16[176,768]{1,0:T(8,128)(2,1)S(1)}, u32[]{:S(2)}, u32[]{:S(2)}) %collective-permute-start) | collective-permute-done | bytes 270368 | tf_op jit(solution)/shard_map/ppermute | solution.py:22
  184.3 1.1 broadcast_in_dim.19
  185.4 5.2 %all-to-all-start = ((bf16[32,176,64]{1,2,0:T(8,128)(2,1)}), bf16[32,176,64]{1,2,0:T(8,128)(2,1)}, u32[]{:S(2)}, u32[]{:S(2)}) async-start(bf16[32,176,64]{1,2,0:T(8,128)(2,1)} %broadcast_in_dim.19), calls=%async_computation | async-start | bytes 2097152 | tf_op jit(solution)/shard_map/all_to_all | solution.py:44
  190.7 2.4 collective-permute-start.8
  193.1 4.0 %collective-permute-done.8 = bf16[176,768]{1,0:T(8,128)(2,1)S(1)} collective-permute-done((bf16[176,768]{1,0:T(8,128)(2,1)S(1)}, bf16[176,768]{1,0:T(8,128)(2,1)S(1)}, u32[]{:S(2)}, u32[]{:S(2)}) %collective-permute-start.8) | collective-permute-done | bytes 270368 | tf_op jit(solution)/shard_map/ppermute | solution.py:24
  197.0 3.4 %collective-permute-start.9 = (bf16[176,768]{1,0:T(8,128)(2,1)S(1)}, bf16[176,768]{1,0:T(8,128)(2,1)S(1)}, u32[]{:S(2)}, u32[]{:S(2)}) collective-permute-start(bf16[176,768]{1,0:T(8,128)(2,1)S(1)} %collective-permute-done.8), channel_id=1, source_target_pairs={{0,480},{32,0},{64,32},{96,64},{128,96},{160,128},{192,160},{224,1... | collective-permute-start | bytes 811016 | tf_op jit(solution)/shard_map/ppermute | solution.py:24
  200.4 4.0 %collective-permute-done.9 = bf16[176,768]{1,0:T(8,128)(2,1)S(1)} collective-permute-done((bf16[176,768]{1,0:T(8,128)(2,1)S(1)}, bf16[176,768]{1,0:T(8,128)(2,1)S(1)}, u32[]{:S(2)}, u32[]{:S(2)}) %collective-permute-start.9) | collective-permute-done | bytes 270368 | tf_op jit(solution)/shard_map/ppermute | solution.py:24
  205.1 3.5 %collective-permute-start.10 = (bf16[176,768]{1,0:T(8,128)(2,1)S(1)}, bf16[176,768]{1,0:T(8,128)(2,1)}, u32[]{:S(2)}, u32[]{:S(2)}) collective-permute-start(bf16[176,768]{1,0:T(8,128)(2,1)S(1)} %collective-permute-done.9), channel_id=1, source_target_pairs={{0,480},{32,0},{64,32},{96,64},{128,96},{160,128},{192,160},{224,1... | collective-permute-start | bytes 811016 | tf_op jit(solution)/shard_map/ppermute | solution.py:24
  208.6 4.0 %collective-permute-done.10 = bf16[176,768]{1,0:T(8,128)(2,1)} collective-permute-done((bf16[176,768]{1,0:T(8,128)(2,1)S(1)}, bf16[176,768]{1,0:T(8,128)(2,1)}, u32[]{:S(2)}, u32[]{:S(2)}) %collective-permute-start.10) | collective-permute-done | bytes 270368 | tf_op jit(solution)/shard_map/ppermute | solution.py:24
  212.6 3.5 %collective-permute-start.11 = (bf16[176,768]{1,0:T(8,128)(2,1)}, bf16[176,768]{1,0:T(8,128)(2,1)}, u32[]{:S(2)}, u32[]{:S(2)}) collective-permute-start(bf16[176,768]{1,0:T(8,128)(2,1)} %collective-permute-done.10), channel_id=1, source_target_pairs={{0,480},{32,0},{64,32},{96,64},{128,96},{160,128},{192,160},{224,1... | collective-permute-start | bytes 811016 | tf_op jit(solution)/shard_map/ppermute | solution.py:24
  216.2 2.9 scatter_custom_fusion.1
  219.1 3.1 scatter_custom_fusion.2
  222.3 2.9 collective-permute-start.12
  225.2 2.6 fusion.28
  227.8 1.7 collective-permute-done.12
  229.5 3.1 collective-permute-start.13
  232.6 4.6 %convolution_convert_fusion = bf16[384,2048]{1,0:T(8,128)(2,1)} fusion(bf16[176,2048]{0,1:T(8,128)(2,1)} %bitcast.1, bf16[384,2048]{1,0:T(8,128)(2,1)S(1)} %fusion.2, bf16[2048,352]{1,0:T(8,128)(2,1)} %all-gather.5.cloned.1.call-done, f32[384,176]{0,1:T(8,128)} %fusion.28), kind=kOutput, calls=%fused_computation.11 | convolution fusion | flops 554840064 | bytes 5513216 | tf_op jit(solution)/shard_map/dot_general | solution.py:83
  237.3 2.7 copy.26
  240.0 3.0 collective-permute-start.14
  243.9 1.0 constant_dynamic-update-slice_fusion.30
  244.9 1.0 constant_dynamic-update-slice_fusion.29
  245.9 1.0 constant_dynamic-update-slice_fusion.28
  246.9 1.0 constant_dynamic-update-slice_fusion.27
  247.8 1.0 constant_dynamic-update-slice_fusion.26
  249.0 1.0 constant_dynamic-update-slice_fusion.20
  249.9 1.0 constant_dynamic-update-slice_fusion.19
  250.9 1.0 constant_dynamic-update-slice_fusion.18
  252.9 1.0 constant_dynamic-update-slice_fusion.15
  253.9 1.0 constant_dynamic-update-slice_fusion.14
  258.0 1.0 constant_dynamic-update-slice_fusion.3
  259.0 1.0 constant_dynamic-update-slice_fusion.2
  260.0 1.0 constant_dynamic-update-slice_fusion.1
  263.4 9.9 %all-to-all-start.3 = ((bf16[2,32,24,128]{3,2,0,1:T(8,128)(2,1)}), bf16[2,32,24,128]{3,2,0,1:T(8,128)(2,1)S(1)}, u32[]{:S(2)}, u32[]{:S(2)}) async-start(bf16[2,32,24,128]{3,2,0,1:T(8,128)(2,1)} %pad_maximum_fusion), calls=%async_computation.3 | async-start | bytes 786432 | tf_op jit(solution)/shard_map/all_to_all | solution.py:137
  273.4 29.3 %reduce-scatter.4.cloned.1.call-done = bf16[128,384]{1,0:T(8,128)(2,1)} async-done(((bf16[2048,384]{1,0:T(8,128)(2,1)}), bf16[128,384]{1,0:T(8,128)(2,1)}) %reduce-scatter.4.cloned.1.call-update) | async-done | bytes 98320
  302.7 1.0 copy.27
  303.7 1.2 fusion.25
  (102 shorter events, 13.2 us)
Async XLA Ops:
  7.4 157.6 %copy-start = (bf16[1,1,176,2048]{3,2,1,0:T(8,128)(2,1)S(1)}, bf16[1,1,176,2048]{3,2,1,0:T(8,128)(2,1)}, u32[]{:S(2)}) copy-start(bf16[1,1,176,2048]{3,2,1,0:T(8,128)(2,1)} %param.15) | copy-start | bytes 2162692
  7.4 67.0 %copy-start.10 = (f32[2048]{0:T(1024)S(1)}, f32[2048]{0:T(1024)}, u32[]{:S(2)}) copy-start(f32[2048]{0:T(1024)} %param.11) | copy-start | bytes 24580
  7.4 65.2 %all-gather.3.cloned.1.call-start = ((), (), s32[]{:S(2)}) async-start(), calls=%async_computation.5 | async-start | bytes 1671168 | tf_op jit(solution)/shard_map/all_gather | solution.py:75
  53.1 18.1 %all-to-all-start.1 = ((s32[2,32,24]{2,0,1:T(2,128)}), s32[2,32,24]{2,0,1:T(2,128)S(1)}, u32[]{:S(2)}, u32[]{:S(2)}) async-start(s32[2,32,24]{2,0,1:T(2,128)} %copy.21), calls=%async_computation.1 | async-start | bytes 65536 | tf_op jit(solution)/shard_map/all_to_all | solution.py:107
  80.5 10.6 %copy-start.7 = (bf16[64,176]{1,0:T(8,128)(2,1)S(1)}, bf16[64,176]{1,0:T(8,128)(2,1)}, u32[]{:S(2)}) copy-start(bf16[64,176]{1,0:T(8,128)(2,1)} %param.13) | copy-start | bytes 67588
  80.5 10.6 %copy-start.8 = (bf16[64,176]{1,0:T(8,128)(2,1)S(1)}, bf16[64,176]{1,0:T(8,128)(2,1)}, u32[]{:S(2)}) copy-start(bf16[64,176]{1,0:T(8,128)(2,1)} %param.12) | copy-start | bytes 67588
  84.4 80.6 %all-to-all-start.2 = ((bf16[32,24,2048]{2,1,0:T(8,128)(2,1)}), bf16[32,24,2048]{2,1,0:T(8,128)(2,1)}, u32[]{:S(2)}, u32[]{:S(2)}) async-start(bf16[32,24,2048]{2,1,0:T(8,128)(2,1)} %broadcast_select_fusion), calls=%async_computation.2 | async-start | bytes 6291456 | tf_op jit(solution)/shard_map/all_to_all | solution.py:112
  91.0 93.2 %copy-start.9 = (bf16[176,64]{0,1:T(8,128)(2,1)S(1)}, bf16[176,64]{0,1:T(8,128)(2,1)}, u32[]{:S(2)}) copy-start(bf16[176,64]{0,1:T(8,128)(2,1)} %param.14) | copy-start | bytes 67588
  91.0 134.2 %all-gather.5.cloned.1.call-start = ((), (), s32[]{:S(2)}) async-start(), calls=%async_computation.6 | async-start | bytes 1622016 | tf_op jit(solution)/shard_map/all_gather | solution.py:35
  164.9 51.2 %copy-start.11 = (f32[2,384]{1,0:T(2,128)S(1)}, f32[2,384]{1,0:T(2,128)}, u32[]{:S(2)}) copy-start(f32[2,384]{1,0:T(2,128)} %param.19) | copy-start | bytes 9220
  171.3 12.9 %collective-permute-start = (bf16[176,768]{1,0:T(8,128)(2,1)S(1)}, bf16[176,768]{1,0:T(8,128)(2,1)S(1)}, u32[]{:S(2)}, u32[]{:S(2)}) collective-permute-start(bf16[176,768]{1,0:T(8,128)(2,1)S(1)} %fusion.9), channel_id=1, source_target_pairs={{0,32},{32,64},{64,96},{96,128},{128,160},{160,192},{192,224},{224... | collective-permute-start | bytes 811016 | tf_op jit(solution)/shard_map/ppermute | solution.py:22
  184.3 8.8 %collective-permute-start.1 = (bf16[176,768]{1,0:T(8,128)(2,1)S(1)}, bf16[176,768]{1,0:T(8,128)(2,1)S(1)}, u32[]{:S(2)}, u32[]{:S(2)}) collective-permute-start(bf16[176,768]{1,0:T(8,128)(2,1)S(1)} %collective-permute-done), channel_id=1, source_target_pairs={{0,32},{32,64},{64,96},{96,128},{128,160},{160,192},{192,224},{224... | collective-permute-start | bytes 811016 | tf_op jit(solution)/shard_map/ppermute | solution.py:22
  185.4 47.2 %all-to-all-start = ((bf16[32,176,64]{1,2,0:T(8,128)(2,1)}), bf16[32,176,64]{1,2,0:T(8,128)(2,1)}, u32[]{:S(2)}, u32[]{:S(2)}) async-start(bf16[32,176,64]{1,2,0:T(8,128)(2,1)} %broadcast_in_dim.19), calls=%async_computation | async-start | bytes 2097152 | tf_op jit(solution)/shard_map/all_to_all | solution.py:44
  190.6 112.1 %reduce-scatter.4.cloned.1.call-start = ((), (), s32[]{:S(2)}) async-start(), calls=%async_computation.7 | async-start | bytes 1671168
  190.7 6.4 %collective-permute-start.8 = (bf16[176,768]{1,0:T(8,128)(2,1)S(1)}, bf16[176,768]{1,0:T(8,128)(2,1)S(1)}, u32[]{:S(2)}, u32[]{:S(2)}) collective-permute-start(bf16[176,768]{1,0:T(8,128)(2,1)S(1)} %fusion.9), channel_id=1, source_target_pairs={{0,480},{32,0},{64,32},{96,64},{128,96},{160,128},{192,160},{224,1... | collective-permute-start | bytes 811016 | tf_op jit(solution)/shard_map/ppermute | solution.py:24
  193.1 7.3 %collective-permute-start.2 = (bf16[176,768]{1,0:T(8,128)(2,1)S(1)}, bf16[176,768]{1,0:T(8,128)(2,1)S(1)}, u32[]{:S(2)}, u32[]{:S(2)}) collective-permute-start(bf16[176,768]{1,0:T(8,128)(2,1)S(1)} %collective-permute-done.1), channel_id=1, source_target_pairs={{0,32},{32,64},{64,96},{96,128},{128,160},{160,192},{192,224},{224... | collective-permute-start | bytes 811016 | tf_op jit(solution)/shard_map/ppermute | solution.py:22
  197.0 7.3 %collective-permute-start.9 = (bf16[176,768]{1,0:T(8,128)(2,1)S(1)}, bf16[176,768]{1,0:T(8,128)(2,1)S(1)}, u32[]{:S(2)}, u32[]{:S(2)}) collective-permute-start(bf16[176,768]{1,0:T(8,128)(2,1)S(1)} %collective-permute-done.8), channel_id=1, source_target_pairs={{0,480},{32,0},{64,32},{96,64},{128,96},{160,128},{192,160},{224,1... | collective-permute-start | bytes 811016 | tf_op jit(solution)/shard_map/ppermute | solution.py:24
  200.4 12.2 %copy-start.3 = (bf16[176,768]{1,0:T(8,128)(2,1)}, bf16[176,768]{1,0:T(8,128)(2,1)S(1)}, u32[]{:S(2)}) copy-start(bf16[176,768]{1,0:T(8,128)(2,1)S(1)} %collective-permute-done.2) | copy-start | bytes 811012
  200.4 8.2 %collective-permute-start.3 = (bf16[176,768]{1,0:T(8,128)(2,1)S(1)}, bf16[176,768]{1,0:T(8,128)(2,1)S(1)}, u32[]{:S(2)}, u32[]{:S(2)}) collective-permute-start(bf16[176,768]{1,0:T(8,128)(2,1)S(1)} %collective-permute-done.2), channel_id=1, source_target_pairs={{0,32},{32,64},{64,96},{96,128},{128,160},{160,192},{192,224},{224... | collective-permute-start | bytes 811016 | tf_op jit(solution)/shard_map/ppermute | solution.py:22
  204.4 0.7 copy-start.1
  205.1 7.5 %collective-permute-start.10 = (bf16[176,768]{1,0:T(8,128)(2,1)S(1)}, bf16[176,768]{1,0:T(8,128)(2,1)}, u32[]{:S(2)}, u32[]{:S(2)}) collective-permute-start(bf16[176,768]{1,0:T(8,128)(2,1)S(1)} %collective-permute-done.9), channel_id=1, source_target_pairs={{0,480},{32,0},{64,32},{96,64},{128,96},{160,128},{192,160},{224,1... | collective-permute-start | bytes 811016 | tf_op jit(solution)/shard_map/ppermute | solution.py:24
  208.6 7.5 %copy-start.5 = (bf16[176,768]{1,0:T(8,128)(2,1)}, bf16[176,768]{1,0:T(8,128)(2,1)S(1)}, u32[]{:S(2)}) copy-start(bf16[176,768]{1,0:T(8,128)(2,1)S(1)} %collective-permute-done.3) | copy-start | bytes 811012
  208.6 7.5 %collective-permute-start.4 = (bf16[176,768]{1,0:T(8,128)(2,1)S(1)}, bf16[176,768]{1,0:T(8,128)(2,1)}, u32[]{:S(2)}, u32[]{:S(2)}) collective-permute-start(bf16[176,768]{1,0:T(8,128)(2,1)S(1)} %collective-permute-done.3), channel_id=1, source_target_pairs={{0,32},{32,64},{64,96},{96,128},{128,160},{160,192},{192,224},{224... | collective-permute-start | bytes 811016 | tf_op jit(solution)/shard_map/ppermute | solution.py:22
  212.6 9.7 %collective-permute-start.11 = (bf16[176,768]{1,0:T(8,128)(2,1)}, bf16[176,768]{1,0:T(8,128)(2,1)}, u32[]{:S(2)}, u32[]{:S(2)}) collective-permute-start(bf16[176,768]{1,0:T(8,128)(2,1)} %collective-permute-done.10), channel_id=1, source_target_pairs={{0,480},{32,0},{64,32},{96,64},{128,96},{160,128},{192,160},{224,1... | collective-permute-start | bytes 811016 | tf_op jit(solution)/shard_map/ppermute | solution.py:24
  216.1 9.1 %collective-permute-start.5 = (bf16[176,768]{1,0:T(8,128)(2,1)}, bf16[176,768]{1,0:T(8,128)(2,1)}, u32[]{:S(2)}, u32[]{:S(2)}) collective-permute-start(bf16[176,768]{1,0:T(8,128)(2,1)} %collective-permute-done.4), channel_id=1, source_target_pairs={{0,32},{32,64},{64,96},{96,128},{128,160},{160,192},{192,224},{224... | collective-permute-start | bytes 811016 | tf_op jit(solution)/shard_map/ppermute | solution.py:22
  222.3 7.2 %collective-permute-start.12 = (bf16[176,768]{1,0:T(8,128)(2,1)}, bf16[176,768]{1,0:T(8,128)(2,1)}, u32[]{:S(2)}, u32[]{:S(2)}) collective-permute-start(bf16[176,768]{1,0:T(8,128)(2,1)} %collective-permute-done.11), channel_id=1, source_target_pairs={{0,480},{32,0},{64,32},{96,64},{128,96},{160,128},{192,160},{224,1... | collective-permute-start | bytes 811016 | tf_op jit(solution)/shard_map/ppermute | solution.py:24
  225.2 7.4 %collective-permute-start.6 = (bf16[176,768]{1,0:T(8,128)(2,1)}, bf16[176,768]{1,0:T(8,128)(2,1)}, u32[]{:S(2)}, u32[]{:S(2)}) collective-permute-start(bf16[176,768]{1,0:T(8,128)(2,1)} %collective-permute-done.5), channel_id=1, source_target_pairs={{0,32},{32,64},{64,96},{96,128},{128,160},{160,192},{192,224},{224... | collective-permute-start | bytes 811016 | tf_op jit(solution)/shard_map/ppermute | solution.py:22
  229.5 10.5 %collective-permute-start.13 = (bf16[176,768]{1,0:T(8,128)(2,1)}, bf16[176,768]{1,0:T(8,128)(2,1)}, u32[]{:S(2)}, u32[]{:S(2)}) collective-permute-start(bf16[176,768]{1,0:T(8,128)(2,1)} %collective-permute-done.12), channel_id=1, source_target_pairs={{0,480},{32,0},{64,32},{96,64},{128,96},{160,128},{192,160},{224,1... | collective-permute-start | bytes 811016 | tf_op jit(solution)/shard_map/ppermute | solution.py:24
  232.6 10.4 %collective-permute-start.7 = (bf16[176,768]{1,0:T(8,128)(2,1)}, bf16[176,768]{1,0:T(8,128)(2,1)}, u32[]{:S(2)}, u32[]{:S(2)}) collective-permute-start(bf16[176,768]{1,0:T(8,128)(2,1)} %collective-permute-done.6), channel_id=1, source_target_pairs={{0,32},{32,64},{64,96},{96,128},{128,160},{160,192},{192,224},{224... | collective-permute-start | bytes 811016 | tf_op jit(solution)/shard_map/ppermute | solution.py:22
  237.2 11.7 %copy-start.2 = (bf16[176,768]{1,0:T(8,128)(2,1)S(1)}, bf16[176,768]{1,0:T(8,128)(2,1)}, u32[]{:S(2)}) copy-start(bf16[176,768]{1,0:T(8,128)(2,1)} %copy-done.1) | copy-start | bytes 811012
  237.2 19.6 %copy-start.6 = (bf16[176,768]{1,0:T(8,128)(2,1)S(1)}, bf16[176,768]{1,0:T(8,128)(2,1)}, u32[]{:S(2)}) copy-start(bf16[176,768]{1,0:T(8,128)(2,1)} %copy-done.5) | copy-start | bytes 811012
  237.3 19.6 %copy-start.4 = (bf16[176,768]{1,0:T(8,128)(2,1)S(1)}, bf16[176,768]{1,0:T(8,128)(2,1)}, u32[]{:S(2)}) copy-start(bf16[176,768]{1,0:T(8,128)(2,1)} %copy-done.3) | copy-start | bytes 811012
  240.0 21.0 %copy-start.12 = (bf16[2,1408,128]{2,1,0:T(8,128)(2,1)S(1)}, bf16[2,1408,128]{2,1,0:T(8,128)(2,1)}, u32[]{:S(2)}) copy-start(bf16[2,1408,128]{2,1,0:T(8,128)(2,1)} %param.17) | copy-start | bytes 2162692
  240.0 12.9 %collective-permute-start.14 = (bf16[176,768]{1,0:T(8,128)(2,1)}, bf16[176,768]{1,0:T(8,128)(2,1)S(1)}, u32[]{:S(2)}, u32[]{:S(2)}) collective-permute-start(bf16[176,768]{1,0:T(8,128)(2,1)} %collective-permute-done.13), channel_id=1, source_target_pairs={{0,480},{32,0},{64,32},{96,64},{128,96},{160,128},{192,160},{224,1... | collective-permute-start | bytes 811016 | tf_op jit(solution)/shard_map/ppermute | solution.py:24
  263.4 40.3 %all-to-all-start.3 = ((bf16[2,32,24,128]{3,2,0,1:T(8,128)(2,1)}), bf16[2,32,24,128]{3,2,0,1:T(8,128)(2,1)S(1)}, u32[]{:S(2)}, u32[]{:S(2)}) async-start(bf16[2,32,24,128]{3,2,0,1:T(8,128)(2,1)} %pad_maximum_fusion), calls=%async_computation.3 | async-start | bytes 786432 | tf_op jit(solution)/shard_map/all_to_all | solution.py:137
Sparse Core Ops, SparseCore 0:
  10.2 46.8 all-gather.2
  240.1 62.5 reduce-scatter.3
Sparse Core Ops, SparseCore 1:
  94.7 91.6 all-gather.4
